TPU v7x, 32 devices: a whole 2x2x4 slice. The times are simulated.
32 devices in a mesh: band: 8 (over y, x, core), gblk: 4 (over z).
Axes of the slice: x: 2, y: 2, z: 4, core: 2. Of those that a mesh axis runs over, the one named last changes fastest.
Arguments:
- eps_inv: bfloat16 [2, 2, 8, 4, 512, 16384], P(None, None, None, 'gblk', None, 'band'), may hold values from -6 to 6
- pair_elements: bfloat16 [2, 1, 16, 16384], P(None, None, 'band'), may hold values from -0.046875 to 0.046875
Outputs:
- sigma_terms: float32 [2, 2, 1, 16], P(None, None, None, 'band')
All inputs are finite; a program needn't handle non-finite values.
Results may differ from a plain program's by a relative error of at most 0.0003.
Values may be sent and summed in bfloat16 or wider, within the bound.
No kernel may reach another device: no remote copies, remote signals or barrier semaphores. Data moves between devices by JAX's collectives and lax.ppermute only.
A program may use at most 128 MiB of HBM per device.

v0:
```python
import jax
import jax.numpy as jnp
from jax import lax
from jax.sharding import PartitionSpec as P


def shards(eps_inv, pair_elements):
    group_count = lax.axis_size("gblk")
    group_index = lax.axis_index("gblk")
    freqs = eps_inv.shape[0]
    rounds = eps_inv.shape[2]
    tile_rows = eps_inv.shape[4]
    width = eps_inv.shape[5]
    states = pair_elements.shape[1]
    local_bands = pair_elements.shape[2]
    columns = lax.all_to_all(pair_elements, "band", split_axis=3, concat_axis=2, tiled=True)
    all_bands = columns.shape[2]
    blocks = eps_inv.reshape(freqs, 2, -1, width)
    shaped = pair_elements.reshape(2, states, local_bands, rounds, group_count, tile_rows)
    picked = lax.dynamic_slice_in_dim(shaped, group_index, 1, 4)
    row_local = picked.reshape(2, states, local_bands, rounds * tile_rows)
    flat = columns.reshape(-1, width)
    contract_last = (((1,), (1,)), ((), ()))
    images = []
    for frequency in range(freqs):
        along_a = lax.dot_general(
            flat, blocks[frequency, 0], contract_last, preferred_element_type=jnp.float32
        )
        along_b = lax.dot_general(
            flat, blocks[frequency, 1], contract_last, preferred_element_type=jnp.float32
        )
        along_a = along_a.reshape(2, states, all_bands, -1)
        along_b = along_b.reshape(2, states, all_bands, -1)
        images.append(jnp.stack([along_a[0] - along_b[1], along_a[1] + along_b[0]]))
    image = jnp.stack(images)
    piece = lax.all_gather(row_local, "band", axis=2, tiled=True)
    real_part = piece[0].astype(jnp.float32)
    imag_part = piece[1].astype(jnp.float32)
    sigma_re = jnp.sum(real_part * image[:, 0] + imag_part * image[:, 1], axis=-1)
    sigma_im = jnp.sum(real_part * image[:, 1] - imag_part * image[:, 0], axis=-1)
    partial_sigma = jnp.stack([sigma_re, sigma_im], axis=1)
    reduced = lax.psum_scatter(partial_sigma, "band", scatter_dimension=3, tiled=True)
    return lax.psum(reduced, "gblk")


def solution(mesh):
    placed = (P(None, None, None, "gblk", None, "band"), P(None, None, "band", None))
    return jax.shard_map(
        shards, mesh=mesh, in_specs=placed, out_specs=P(None, None, None, "band"), check_vma=False
    )
```

profile of v0, /device:TPU:0, one launch (start us, length us, event | category | flops | bytes accessed | tf_op | source)
XLA Modules:
  0.0 138.5 jit_solution(16395664978475546550)
XLA Ops:
  0.0 0.0 copy-start.1
  0.0 0.0 copy-start
  0.0 15.4 %copy.24 = bf16[2,1,2,16384]{2,0,1,3:T(2,128)(2,1)} copy(bf16[2,1,2,16384]{3,2,1,0:T(2,128)(2,1)} %param.3) | data formatting | bytes 262144 | tf_op args[1]
  15.5 13.7 %reshape.124 = bf16[8,2,4096]{2,1,0:T(2,128)(2,1)} reshape(bf16[16384,1,2,2]{3,2,1,0:T(2,128)(2,1)} %bitcast.63) | data formatting | bytes 262144
  29.2 5.2 %all-to-all-start = ((bf16[8,2,4096]{2,1,0:T(2,128)(2,1)}), bf16[8,2,4096]{2,1,0:T(2,128)(2,1)S(1)}, u32[]{:S(2)}, u32[]{:S(2)}) async-start(bf16[8,2,4096]{2,1,0:T(2,128)(2,1)} %reshape.124), calls=%async_computation | async-start | bytes 262144 | tf_op jit(solution)/shard_map/all_to_all | solution.py:16
  34.4 0.0 copy-done
  34.4 0.1 reshape.113
  34.5 0.2 dynamic-slice_reduce_fusion
  34.8 9.8 %all_gather.3 = bf16[2,1,16,4096]{3,0,1,2:T(2,128)(2,1)S(1)} all-gather(bf16[2,1,2,4096]{3,0,1,2:T(2,128)(2,1)S(1)} %copy.23), channel_id=1, replica_groups=mesh['band'=8,'gblk'=4] {'band'}, dimensions={2}, use_global_device_ids=true | all-gather | bytes 294912 | tf_op jit(solution)/shard_map/all_gather | solution.py:36
  44.6 0.5 slice_convert_fusion.1
  45.1 0.3 copy_bitcast_fusion
  45.4 0.0 copy-done.1
  45.4 0.6 dynamic-slice
  46.7 0.0 all-to-all-done
  46.7 19.1 %reshape.125 = bf16[16384,1,2,2]{3,2,1,0:T(2,128)(2,1)} reshape(bf16[8,2,4096]{2,1,0:T(2,128)(2,1)S(1)} %all-to-all-done) | data formatting | bytes 262144
  65.8 11.9 %copy.29 = bf16[2,1,2,8,2048]{4,3,2,0,1:T(8,128)(2,1)S(1)} copy(bf16[2,1,2,8,2048]{2,0,4,3,1:T(2,128)(2,1)} %bitcast.62) | data formatting | bytes 262144 | tf_op jit(solution)/shard_map/all_to_all | solution.py:16
  77.6 0.1 copy.26
  77.8 0.1 reshape.115
  77.9 8.6 %fusion.2 = f32[32,4096]{1,0:T(8,128)S(1)} fusion(bf16[32,2048]{1,0:T(8,128)(2,1)S(1)} %reshape.115, bf16[2,2,4096,2048]{3,2,1,0:T(8,128)(2,1)} %bitcast.2), kind=kOutput, calls=%fused_computation.5 | convolution fusion | flops 536870912 | bytes 17432576 | tf_op jit(solution)/shard_map/dot_general | solution.py:29
  86.4 8.6 %fusion.3 = f32[32,4096]{1,0:T(8,128)S(1)} fusion(bf16[32,2048]{1,0:T(8,128)(2,1)S(1)} %reshape.115, bf16[2,2,4096,2048]{3,2,1,0:T(8,128)(2,1)} %bitcast.2), kind=kOutput, calls=%fused_computation.7 | convolution fusion | flops 536870912 | bytes 17432576 | tf_op jit(solution)/shard_map/dot_general | solution.py:26
  95.0 8.6 %fusion = f32[32,4096]{1,0:T(8,128)S(1)} fusion(bf16[32,2048]{1,0:T(8,128)(2,1)S(1)} %reshape.115, bf16[2,2,4096,2048]{3,2,1,0:T(8,128)(2,1)} %bitcast.2), kind=kOutput, calls=%fused_computation.1 | convolution fusion | flops 536870912 | bytes 17432576 | tf_op jit(solution)/shard_map/dot_general | solution.py:29
  103.6 8.6 %fusion.1 = f32[32,4096]{1,0:T(8,128)S(1)} fusion(bf16[32,2048]{1,0:T(8,128)(2,1)S(1)} %reshape.115, bf16[2,2,4096,2048]{3,2,1,0:T(8,128)(2,1)} %bitcast.2), kind=kOutput, calls=%fused_computation.3 | convolution fusion | flops 536870912 | bytes 17432576 | tf_op jit(solution)/shard_map/dot_general | solution.py:26
  112.2 0.1 fusion.10
  112.3 0.1 fusion.8
  112.4 0.2 add_reduce_fusion
  112.7 13.2 %all-reduce = f32[2,2,1,16]{3,0,2,1:T(2,128)S(1)} all-reduce(f32[2,2,1,16]{3,0,2,1:T(2,128)S(1)} %pad_maximum_fusion.1), channel_id=2, replica_groups=mesh['band'=8,'gblk'=4] {'band'}, use_global_device_ids=true, to_apply=%region_2.0.clone | all-reduce | flops 64 | bytes 512
  125.9 0.1 constant_dynamic-slice_fusion
  125.9 11.9 %psum.7 = f32[2,2,1,2]{3,0,2,1:T(2,128)S(1)} all-reduce(f32[2,2,1,2]{3,0,2,1:T(2,128)S(1)} %constant_dynamic-slice_fusion), channel_id=1, replica_groups=mesh['band'=8,'gblk'=4] {'gblk'}, use_global_device_ids=true, to_apply=%region_3.0 | all-reduce | flops 8 | bytes 64 | tf_op jit(solution)/shard_map/psum | solution.py:43
  137.9 0.6 copy.28
  (5 shorter events, 0.1 us)
Async XLA Ops:
  0.0 45.4 %copy-start.1 = (u32[32]{0:T(128)S(1)}, u32[32]{0:T(128)}, u32[]{:S(2)}) copy-start(u32[32]{0:T(128)} %constant.14) | copy-start | bytes 388
  0.0 34.4 %copy-start = (bf16[2,1,2,16384]{3,2,1,0:T(2,128)(2,1)S(1)}, bf16[2,1,2,16384]{3,2,1,0:T(2,128)(2,1)}, u32[]{:S(2)}) copy-start(bf16[2,1,2,16384]{3,2,1,0:T(2,128)(2,1)} %param.3) | copy-start | bytes 393220
  29.2 17.5 %all-to-all-start = ((bf16[8,2,4096]{2,1,0:T(2,128)(2,1)}), bf16[8,2,4096]{2,1,0:T(2,128)(2,1)S(1)}, u32[]{:S(2)}, u32[]{:S(2)}) async-start(bf16[8,2,4096]{2,1,0:T(2,128)(2,1)} %reshape.124), calls=%async_computation | async-start | bytes 262144 | tf_op jit(solution)/shard_map/all_to_all | solution.py:16
where the time goes:
time: 140 us; the launch traced here: 138 us
  local copies, waits for them, and re-layouts  62.2 us (44%)
  blocking collectives  35 us (25%)
  matrix products  34.3 us (24%)
  starting transfers between devices  5.2 us (4%)
    unnamed x10, local copies, waits for them, and re-layouts  49.2 us
    dot_general x2, matrix products, shards(): lax.dot_general(flat, blocks[frequency, 0], contract_last, preferred_elem...  17.2 us
    dot_general x2, matrix products, shards(): lax.dot_general(flat, blocks[frequency, 1], contract_last, preferred_elem...  17.1 us
    unnamed x1, blocking collectives  13.2 us
    all_to_all x2, local copies, waits for them, and re-layouts, shards(): lax.all_to_all(pair_elements, 'band', split_axis=3, concat_axis=2, tiled=...  12 us
    psum x1, blocking collectives, shards(): return lax.psum(reduced, 'gblk')  11.9 us
    all_gather x1, blocking collectives, shards(): piece = lax.all_gather(row_local, 'band', axis=2, tiled=True)  9.81 us
    all_to_all x1, starting transfers between devices, shards(): lax.all_to_all(pair_elements, 'band', split_axis=3, concat_axis=2, tiled=...  5.2 us
  transfers between devices with their start and end apart: 1, of which 0 were waited for; matrix products, arithmetic and copies ran while one was open for 1% of the time, Pallas kernels for 0%

commit v1 on v0

v1 whole, which is shorter than its diff:
```python
import jax
import jax.numpy as jnp
from jax import lax
from jax.experimental import pallas as pl
from jax.experimental.pallas import tpu as pltpu
from jax.sharding import PartitionSpec as P

AXES = ("band", "gblk")


def pack_kernel(pair_ref, cols_ref, rows_ref, *, owners, width, tile_rows, rounds, groups):
    group = lax.axis_index("gblk")
    local = pair_ref.shape[2]
    for part in range(2):
        at = pl.ds(part * local, local)
        for owner in range(owners):
            cols_ref[owner, at, :] = pair_ref[part, 0, :, pl.ds(owner * width, width)]
        for r in range(rounds):
            start = pl.multiple_of((r * groups + group) * tile_rows, tile_rows)
            tile = pair_ref[part, 0, :, pl.ds(start, tile_rows)]
            for owner in range(owners):
                rows_ref[owner, at, pl.ds(r * tile_rows, tile_rows)] = tile


def image_kernel(cols_ref, a0_ref, b0_ref, a1_ref, b1_ref, out_ref, w_ref):
    owners, per, _ = cols_ref.shape
    half = per // 2
    own = owners * per

    @pl.when(pl.program_id(0) == 0)
    def _():
        zero = jnp.zeros((own, cols_ref.shape[2]), w_ref.dtype)
        for copy in range(2):
            for f in range(2):
                base = (2 * copy + f) * own
                w_ref[2 * (1 - f), pl.ds(base, own), :] = zero
                w_ref[2 * (1 - f) + 1, pl.ds(base, own), :] = zero
                for owner in range(owners):
                    re = cols_ref[owner, pl.ds(0, half), :]
                    im = cols_ref[owner, pl.ds(half, half), :]
                    at = base + owner * per
                    w_ref[2 * f, pl.ds(at, half), :] = re
                    w_ref[2 * f, pl.ds(at + half, half), :] = im
                    w_ref[2 * f + 1, pl.ds(at, half), :] = -im
                    w_ref[2 * f + 1, pl.ds(at + half, half), :] = re

    acc = None
    for j, x_ref in enumerate((a0_ref, b0_ref, a1_ref, b1_ref)):
        term = lax.dot_general(
            x_ref[0], w_ref[j], (((1,), (1,)), ((), ())), preferred_element_type=jnp.float32
        )
        acc = term if acc is None else acc + term
    high = acc.astype(jnp.bfloat16).astype(jnp.float32)
    lane = lax.broadcasted_iota(jnp.int32, acc.shape, 1)
    out_ref[...] = jnp.where(lane < acc.shape[1] // 2, high, acc - high).astype(jnp.bfloat16)


def sigma_kernel(rows_ref, image_ref, out_ref, flat_ref, *, groups):
    owners, per, _ = rows_ref.shape
    for owner in range(owners):
        flat_ref[pl.ds(owner * per, per), :] = rows_ref[owner]
    both = jnp.dot(flat_ref[...], image_ref[...], preferred_element_type=jnp.float32)
    for owner in range(owners):
        block = both[owner * per : (owner + 1) * per]
        for group in range(groups):
            out_ref[owner * groups + group] = block


def final_kernel(parts_ref, out_ref):
    _, per, lanes = parts_ref.shape
    half = per // 2
    owner = lax.axis_index("band")
    total = jnp.sum(parts_ref[...], axis=0)
    lane = lax.broadcasted_iota(jnp.int32, (1, lanes), 1)
    own = lanes // 4

    def pick(row, f, slot):
        at = f * own + owner * per + slot
        keep = jnp.logical_or(lane == at, lane == at + 2 * own)
        return jnp.sum(jnp.where(keep, total[row : row + 1], 0.0))

    for f in range(2):
        for l in range(half):
            out_ref[f, 0, 0, l] = pick(l, f, l) + pick(half + l, f, half + l)
            out_ref[f, 1, 0, l] = pick(l, f, half + l) - pick(half + l, f, l)


def shards(eps_inv, pair_elements):
    owners = lax.axis_size("band")
    groups = lax.axis_size("gblk")
    freqs, _, rounds, _, tile_rows, width = eps_inv.shape
    local = pair_elements.shape[2]
    rows = rounds * tile_rows
    per = 2 * local
    lanes = 2 * freqs * owners * per
    vmem = pl.BlockSpec(memory_space=pltpu.VMEM)

    def packing(*refs):
        pack_kernel(*refs, owners=owners, width=width, tile_rows=tile_rows, rounds=rounds, groups=groups)

    cols, picked = pl.pallas_call(
        packing,
        out_shape=(
            jax.ShapeDtypeStruct((owners, per, width), jnp.bfloat16),
            jax.ShapeDtypeStruct((owners, per, rows), jnp.bfloat16),
        ),
        in_specs=[vmem],
        out_specs=(vmem, vmem),
        name="pack",
    )(pair_elements)
    cols = lax.all_to_all(cols, "band", 0, 0, tiled=True)
    picked = lax.all_to_all(picked, "band", 0, 0, tiled=True)

    blocks = eps_inv.reshape(freqs * 2, rows, width)
    bm = min(256, rows)

    def block_of(j):
        return pl.BlockSpec((1, bm, width), lambda i, j=j: (j, i, 0))

    image = pl.pallas_call(
        image_kernel,
        grid=(rows // bm,),
        out_shape=jax.ShapeDtypeStruct((rows, lanes), jnp.bfloat16),
        in_specs=[pl.BlockSpec(cols.shape, lambda i: (0, 0, 0))] + [block_of(j) for j in range(4)],
        out_specs=pl.BlockSpec((bm, lanes), lambda i: (i, 0)),
        scratch_shapes=[pltpu.VMEM((4, lanes, width), jnp.bfloat16)],
        compiler_params=pltpu.CompilerParams(
            dimension_semantics=("arbitrary",), vmem_limit_bytes=40 * 2**20
        ),
        name="image",
    )(cols, blocks, blocks, blocks, blocks)

    def contracting(*refs):
        sigma_kernel(*refs, groups=groups)

    partial = pl.pallas_call(
        contracting,
        out_shape=jax.ShapeDtypeStruct((owners * groups, per, lanes), jnp.float32),
        in_specs=[vmem, vmem],
        out_specs=vmem,
        scratch_shapes=[pltpu.VMEM((owners * per, rows), jnp.bfloat16)],
        name="contract",
    )(picked, image)
    parts = lax.all_to_all(partial, AXES, 0, 0, tiled=True)
    return pl.pallas_call(
        final_kernel,
        out_shape=jax.ShapeDtypeStruct((freqs, 2, 1, local), jnp.float32),
        in_specs=[vmem],
        out_specs=pl.BlockSpec(memory_space=pltpu.SMEM),
        name="final",
    )(parts)


def solution(mesh):
    placed = (P(None, None, None, "gblk", None, "band"), P(None, None, "band", None))
    return jax.shard_map(
        shards, mesh=mesh, in_specs=placed, out_specs=P(None, None, None, "band"), check_vma=False
    )
```

time: 140 us -> 65.9 us (0.47)
  local copies, waits for them, and re-layouts: 62.2 us -> 1.65 us
  Pallas kernels: 0 us -> 35.8 us
  matrix products: 34.3 us -> 0 us
  blocking collectives: 35 us -> 24.5 us
  starting transfers between devices: 5.2 us -> 3.41 us
    unnamed x10 -> x4, local copies, waits for them, and re-layouts: 49.2 us -> 1.65 us
    pallas_call x0 -> x4, Pallas kernels: none -> 35.8 us  [the longest x1 30.3 us: shards(): pl.pallas_call(image_kernel, grid=(rows // bm,), out_shape=jax.ShapeDtype...]
    dot_general x4 -> x0, matrix products: 34.3 us -> none  [the longest x2 17.2 us: shards(): lax.dot_general(flat, blocks[frequency, 0], contract_last, preferred_elem...]
    all_to_all x0 -> x2, blocking collectives: none -> 24.5 us  [the longest x1 13.8 us: shards(): parts = lax.all_to_all(partial, AXES, 0, 0, tiled=True)]
    unnamed x1 -> x0, blocking collectives: 13.2 us -> none
    all_to_all x2 -> x0, local copies, waits for them, and re-layouts: 12 us -> none  [shards(): lax.all_to_all(pair_elements, 'band', split_axis=3, concat_axis=2, tiled=...]
    psum x1 -> x0, blocking collectives: 11.9 us -> none  [shards(): return lax.psum(reduced, 'gblk')]
    all_gather x1 -> x0, blocking collectives: 9.81 us -> none  [shards(): piece = lax.all_gather(row_local, 'band', axis=2, tiled=True)]
  transfers between devices with their start and end apart: 1 -> 1, of which waited for: 0 -> 0; matrix products, arithmetic and copies ran while one was open for 1% -> 0% of each run, Pallas kernels for 0% -> 46%
where the time goes in v1:
time: 65.9 us; the launch traced here: 65.4 us
  Pallas kernels  35.8 us (54%)
  blocking collectives  24.5 us (37%)
  starting transfers between devices  3.41 us (5%)
  local copies, waits for them, and re-layouts  1.65 us (3%)
    pallas_call x1, Pallas kernels, shards(): pl.pallas_call(image_kernel, grid=(rows // bm,), out_shape=jax.ShapeDtype...  30.3 us
    all_to_all x1, blocking collectives, shards(): parts = lax.all_to_all(partial, AXES, 0, 0, tiled=True)  13.8 us
    all_to_all x1, blocking collectives, shards(): cols = lax.all_to_all(cols, 'band', 0, 0, tiled=True)  10.7 us
    all_to_all x1, starting transfers between devices, shards(): picked = lax.all_to_all(picked, 'band', 0, 0, tiled=True)  3.41 us
    pallas_call x1, Pallas kernels, shards(): pl.pallas_call(contracting, out_shape=jax.ShapeDtypeStruct((owners * grou...  2.25 us
    pallas_call x1, Pallas kernels, shards(): pl.pallas_call(packing, out_shape=(jax.ShapeDtypeStruct((owners, per, wid...  1.7 us
    unnamed x4, local copies, waits for them, and re-layouts  1.65 us
    pallas_call x1, Pallas kernels, shards(): pl.pallas_call(final_kernel, out_shape=jax.ShapeDtypeStruct((freqs, 2, 1,...  1.59 us
  transfers between devices with their start and end apart: 1, of which 0 were waited for; matrix products, arithmetic and copies ran while one was open for 0% of the time, Pallas kernels for 46%

profile of v1, /device:TPU:0, one launch (start us, length us, event | category | flops | bytes accessed | tf_op | source)
XLA Modules:
  0.0 65.4 jit_solution(13128631300667249581)
XLA Ops:
  0.0 1.7 %pack.1 = (bf16[8,4,2048]{2,1,0:T(4,128)(2,1)}, bf16[8,4,4096]{2,1,0:T(4,128)(2,1)}) custom-call(bf16[2,1,2,16384]{3,2,1,0:T(2,128)(2,1)} %refs_0_.1), custom_call_target="tpu_custom_call" | custom-call | tf_op jit(solution)/shard_map/pack/pallas_call | solution.py:101
  1.7 10.7 %all_to_all.15.cols_ref = bf16[8,4,2048]{2,1,0:T(4,128)(2,1)S(1)} all-to-all(bf16[8,4,2048]{2,1,0:T(4,128)(2,1)} %get-tuple-element.8), channel_id=1, replica_groups=mesh['band'=8,'gblk'=4] {'band'}, dimensions={0} | all-to-all | bytes 262144 | tf_op jit(solution)/shard_map/all_to_all | solution.py:111
  12.4 3.4 %all-to-all-start = ((bf16[8,4,4096]{2,1,0:T(4,128)(2,1)}), bf16[8,4,4096]{2,1,0:T(4,128)(2,1)S(1)}, u32[]{:S(2)}, u32[]{:S(2)}) async-start(bf16[8,4,4096]{2,1,0:T(4,128)(2,1)} %get-tuple-element.7), calls=%async_computation | async-start | bytes 524288 | tf_op jit(solution)/shard_map/all_to_all | solution.py:112
  15.8 30.3 %image.1.refs_1_ = bf16[4096,128]{1,0:T(8,128)(2,1)S(1)} custom-call(bf16[8,4,2048]{2,1,0:T(4,128)(2,1)S(1)} %all_to_all.15.cols_ref, bf16[4,4096,2048]{2,1,0:T(8,128)(2,1)} %bitcast.a0_ref.b0_ref.a1_ref.b1_ref, bf16[4,4096,2048]{2,1,0:T(8,128)(2,1)} %bitcast.a0_ref.b0_ref.a1_ref.b1_ref, bf16[4,4096,2048]{2,1,0:T(8,128)(2,1)} %bitcast.a0_ref.b0_ref.a1_ref.b1_ref, ...), custom_call_target="tpu_custom_call" | custom-call | tf_op jit(solution)/shard_map/image/pallas_call | solution.py:120
  46.1 0.0 copy-start
  46.1 1.0 %copy-done = bf16[4096,128]{1,0:T(8,128)(2,1)} copy-done((bf16[4096,128]{1,0:T(8,128)(2,1)}, bf16[4096,128]{1,0:T(8,128)(2,1)S(1)}, u32[]{:S(2)}) %copy-start) | copy-done | bytes 1048600
  47.0 0.0 all-to-all-done.refs_0_
  47.0 0.0 copy-start.1
  47.0 0.7 %copy-done.1 = bf16[8,4,4096]{2,1,0:T(4,128)(2,1)} copy-done((bf16[8,4,4096]{2,1,0:T(4,128)(2,1)}, bf16[8,4,4096]{2,1,0:T(4,128)(2,1)S(1)}, u32[]{:S(2)}) %copy-start.1) | copy-done | bytes 262168
  47.7 2.2 %contract.1 = f32[32,4,128]{2,1,0:T(4,128)} custom-call(bf16[8,4,4096]{2,1,0:T(4,128)(2,1)} %copy-done.1, bf16[4096,128]{1,0:T(8,128)(2,1)} %copy-done), custom_call_target="tpu_custom_call" | custom-call | tf_op jit(solution)/shard_map/contract/pallas_call | solution.py:136
  50.0 13.8 %all_to_all.16.parts_ref = f32[32,4,128]{2,1,0:T(4,128)} all-to-all(f32[32,4,128]{2,1,0:T(4,128)} %contract.1), channel_id=1, replica_groups=mesh['band'=8,'gblk'=4] {'band','gblk'}, dimensions={0} | all-to-all | bytes 131072 | tf_op jit(solution)/shard_map/all_to_all | solution.py:144
  63.8 1.6 %final.1 = f32[2,2,1,2]{3,2,1,0:T(1,128)} custom-call(f32[32,4,128]{2,1,0:T(4,128)} %all_to_all.16.parts_ref), custom_call_target="tpu_custom_call" | custom-call | tf_op jit(solution)/shard_map/final/pallas_call | solution.py:145
Async XLA Ops:
  12.4 34.7 %all-to-all-start = ((bf16[8,4,4096]{2,1,0:T(4,128)(2,1)}), bf16[8,4,4096]{2,1,0:T(4,128)(2,1)S(1)}, u32[]{:S(2)}, u32[]{:S(2)}) async-start(bf16[8,4,4096]{2,1,0:T(4,128)(2,1)} %get-tuple-element.7), calls=%async_computation | async-start | bytes 524288 | tf_op jit(solution)/shard_map/all_to_all | solution.py:112
  46.1 1.0 %copy-start = (bf16[4096,128]{1,0:T(8,128)(2,1)}, bf16[4096,128]{1,0:T(8,128)(2,1)S(1)}, u32[]{:S(2)}) copy-start(bf16[4096,128]{1,0:T(8,128)(2,1)S(1)} %image.1.refs_1_) | copy-start | bytes 3145732
  47.0 0.7 %copy-start.1 = (bf16[8,4,4096]{2,1,0:T(4,128)(2,1)}, bf16[8,4,4096]{2,1,0:T(4,128)(2,1)S(1)}, u32[]{:S(2)}) copy-start(bf16[8,4,4096]{2,1,0:T(4,128)(2,1)S(1)} %all-to-all-done.refs_0_) | copy-start | bytes 786436

commit v2 on v1

v2 whole, which is shorter than its diff:
```python
import jax
import jax.numpy as jnp
from jax import lax
from jax.experimental import pallas as pl
from jax.experimental.pallas import tpu as pltpu
from jax.sharding import PartitionSpec as P

AXES = ("band", "gblk")
BM = 1024


def pack_kernel(pair_ref, out_ref, *, owners, width, tile_rows, rounds, groups):
    group = lax.axis_index("gblk")
    local = pair_ref.shape[2]
    for part in range(2):
        at = pl.ds(part * local, local)
        for owner in range(owners):
            out_ref[owner, at, pl.ds(0, width)] = pair_ref[part, 0, :, pl.ds(owner * width, width)]
        for r in range(rounds):
            start = pl.multiple_of((r * groups + group) * tile_rows, tile_rows)
            tile = pair_ref[part, 0, :, pl.ds(start, tile_rows)]
            for owner in range(owners):
                out_ref[owner, at, pl.ds(width + r * tile_rows, tile_rows)] = tile


def image_kernel(pair_ref, a_ref, b_ref, out_ref, w_ref, flat_ref, sum_ref, *, width, groups):
    owners, per, _ = pair_ref.shape
    half = per // 2
    own = owners * per
    step = pl.program_id(0)
    steps = pl.num_programs(0)
    freqs = w_ref.shape[0] // 2
    bm = a_ref.shape[1]
    rows = flat_ref.shape[1]
    now = step // (rows // bm)

    @pl.when(step == 0)
    def _():
        sum_ref[...] = jnp.zeros_like(sum_ref)
        zero = jnp.zeros((own, width), w_ref.dtype)
        for copy in range(2):
            for f in range(freqs):
                base = (copy * freqs + f) * own
                for other in range(freqs):
                    if other != f:
                        w_ref[2 * other, pl.ds(base, own), :] = zero
                        w_ref[2 * other + 1, pl.ds(base, own), :] = zero
                for owner in range(owners):
                    re = pair_ref[owner, pl.ds(0, half), pl.ds(0, width)]
                    im = pair_ref[owner, pl.ds(half, half), pl.ds(0, width)]
                    at = base + owner * per
                    w_ref[2 * f, pl.ds(at, half), :] = re
                    w_ref[2 * f, pl.ds(at + half, half), :] = im
                    w_ref[2 * f + 1, pl.ds(at, half), :] = -im
                    w_ref[2 * f + 1, pl.ds(at + half, half), :] = re
        for owner in range(owners):
            flat_ref[pl.ds(owner * per, per), :] = pair_ref[owner, :, pl.ds(width, rows)]

    acc = None
    for part, block_ref in enumerate((a_ref, b_ref)):
        term = lax.dot_general(
            block_ref[0], w_ref[2 * now + part], (((1,), (1,)), ((), ())),
            preferred_element_type=jnp.float32,
        )
        acc = term if acc is None else acc + term
    high = acc.astype(jnp.bfloat16).astype(jnp.float32)
    lane = lax.broadcasted_iota(jnp.int32, acc.shape, 1)
    image = jnp.where(lane < acc.shape[1] // 2, high, acc - high).astype(jnp.bfloat16)
    at = pl.multiple_of((step % (rows // bm)) * bm, bm)
    sum_ref[...] += jnp.dot(flat_ref[:, pl.ds(at, bm)], image, preferred_element_type=jnp.float32)

    @pl.when(step == steps - 1)
    def _():
        for owner in range(owners):
            block = sum_ref[pl.ds(owner * per, per), :]
            for group in range(groups):
                out_ref[owner * groups + group] = block


def final_kernel(parts_ref, out_ref):
    _, per, lanes = parts_ref.shape
    half = per // 2
    owner = lax.axis_index("band")
    total = jnp.sum(parts_ref[...], axis=0)
    lane = lax.broadcasted_iota(jnp.int32, (1, lanes), 1)
    freqs = out_ref.shape[0]
    own = lanes // (2 * freqs)

    def pick(row, f, slot):
        at = f * own + owner * per + slot
        keep = jnp.logical_or(lane == at, lane == at + freqs * own)
        return jnp.sum(jnp.where(keep, total[row : row + 1], 0.0))

    for f in range(freqs):
        for l in range(half):
            out_ref[f, 0, 0, l] = pick(l, f, l) + pick(half + l, f, half + l)
            out_ref[f, 1, 0, l] = pick(l, f, half + l) - pick(half + l, f, l)


def shards(eps_inv, pair_elements):
    owners = lax.axis_size("band")
    groups = lax.axis_size("gblk")
    freqs, _, rounds, _, tile_rows, width = eps_inv.shape
    local = pair_elements.shape[2]
    rows = rounds * tile_rows
    per = 2 * local
    lanes = 2 * freqs * owners * per
    vmem = pl.BlockSpec(memory_space=pltpu.VMEM)

    def packing(*refs):
        pack_kernel(*refs, owners=owners, width=width, tile_rows=tile_rows, rounds=rounds, groups=groups)

    packed = pl.pallas_call(
        packing,
        out_shape=jax.ShapeDtypeStruct((owners, per, width + rows), jnp.bfloat16),
        in_specs=[vmem],
        out_specs=vmem,
        name="pack",
    )(pair_elements)
    spread = lax.all_to_all(packed, "band", 0, 0, tiled=True)

    blocks = eps_inv.reshape(freqs * 2, rows, width)
    bm = min(BM, rows)
    steps = rows // bm

    def block_of(part):
        return pl.BlockSpec((1, bm, width), lambda i: (2 * (i // steps) + part, i % steps, 0))

    def imaging(*refs):
        image_kernel(*refs, width=width, groups=groups)

    partial = pl.pallas_call(
        imaging,
        grid=(freqs * steps,),
        out_shape=jax.ShapeDtypeStruct((owners * groups, per, lanes), jnp.float32),
        in_specs=[vmem] + [block_of(0), block_of(1)],
        out_specs=vmem,
        scratch_shapes=[
            pltpu.VMEM((2 * freqs, lanes, width), jnp.bfloat16),
            pltpu.VMEM((owners * per, rows), jnp.bfloat16),
            pltpu.VMEM((owners * per, lanes), jnp.float32),
        ],
        compiler_params=pltpu.CompilerParams(
            dimension_semantics=("arbitrary",), vmem_limit_bytes=40 * 2**20
        ),
        name="image",
    )(spread, blocks, blocks)
    parts = lax.all_to_all(partial, AXES, 0, 0, tiled=True)
    return pl.pallas_call(
        final_kernel,
        out_shape=jax.ShapeDtypeStruct((freqs, 2, 1, local), jnp.float32),
        in_specs=[vmem],
        out_specs=pl.BlockSpec(memory_space=pltpu.SMEM),
        name="final",
    )(parts)


def solution(mesh):
    placed = (P(None, None, None, "gblk", None, "band"), P(None, None, "band", None))
    return jax.shard_map(
        shards, mesh=mesh, in_specs=placed, out_specs=P(None, None, None, "band"), check_vma=False
    )
```

time: 65.9 us -> 56 us (0.85)
  Pallas kernels: 35.8 us -> 30.8 us
  starting transfers between devices: 3.41 us -> 0 us
  local copies, waits for them, and re-layouts: 1.65 us -> 0 us
    pallas_call x3 -> x2, Pallas kernels: 34.2 us -> 29.2 us  [the longest x1 27.5 us: shards(): pl.pallas_call(imaging, grid=(freqs * steps,), out_shape=jax.ShapeDtypeSt...]
    all_to_all x1 -> x0, starting transfers between devices: 3.41 us -> none  [shards(): picked = lax.all_to_all(picked, 'band', 0, 0, tiled=True)]
    all_to_all x1, blocking collectives: 10.7 us -> 13.5 us  [shards(): spread = lax.all_to_all(packed, 'band', 0, 0, tiled=True)]
    all_to_all x1, blocking collectives: 13.8 us -> 11.4 us  [shards(): parts = lax.all_to_all(partial, AXES, 0, 0, tiled=True)]
    unnamed x4 -> x0, local copies, waits for them, and re-layouts: 1.65 us -> none
  transfers between devices with their start and end apart: 1 -> 0, of which waited for: 0 -> 0; matrix products, arithmetic and copies ran while one was open for 0% -> 0% of each run, Pallas kernels for 46% -> 0%
where the time goes in v2:
time: 56 us; the launch traced here: 55.7 us
  Pallas kernels  30.8 us (55%)
  blocking collectives  24.9 us (44%)
    pallas_call x1, Pallas kernels, shards(): pl.pallas_call(imaging, grid=(freqs * steps,), out_shape=jax.ShapeDtypeSt...  27.5 us
    all_to_all x1, blocking collectives, shards(): spread = lax.all_to_all(packed, 'band', 0, 0, tiled=True)  13.5 us
    all_to_all x1, blocking collectives, shards(): parts = lax.all_to_all(partial, AXES, 0, 0, tiled=True)  11.4 us
    pallas_call x1, Pallas kernels, shards(): pl.pallas_call(packing, out_shape=jax.ShapeDtypeStruct((owners, per, widt...  1.73 us
    pallas_call x1, Pallas kernels, shards(): pl.pallas_call(final_kernel, out_shape=jax.ShapeDtypeStruct((freqs, 2, 1,...  1.59 us

profile of v2, /device:TPU:0, one launch (start us, length us, event | category | flops | bytes accessed | tf_op | source)
XLA Modules:
  0.0 55.7 jit_solution(17684135360869746119)
XLA Ops:
  0.0 1.7 %pack.1 = bf16[8,4,6144]{2,1,0:T(4,128)(2,1)} custom-call(bf16[2,1,2,16384]{3,2,1,0:T(2,128)(2,1)} %refs_0_.1), custom_call_target="tpu_custom_call" | custom-call | tf_op jit(solution)/shard_map/pack/pallas_call | solution.py:113
  1.7 13.5 %all_to_all.10.refs_0_ = bf16[8,4,6144]{2,1,0:T(4,128)(2,1)S(1)} all-to-all(bf16[8,4,6144]{2,1,0:T(4,128)(2,1)} %pack.1), channel_id=1, replica_groups=mesh['band'=8,'gblk'=4] {'band'}, dimensions={0} | all-to-all | bytes 786432 | tf_op jit(solution)/shard_map/all_to_all | solution.py:120
  15.2 27.5 %image.1 = f32[32,4,128]{2,1,0:T(4,128)S(1)} custom-call(bf16[8,4,6144]{2,1,0:T(4,128)(2,1)S(1)} %all_to_all.10.refs_0_, bf16[4,4096,2048]{2,1,0:T(8,128)(2,1)} %bitcast.refs_1_.refs_2_, bf16[4,4096,2048]{2,1,0:T(8,128)(2,1)} %bitcast.refs_1_.refs_2_), custom_call_target="tpu_custom_call" | custom-call | tf_op jit(solution)/shard_map/image/pallas_call | solution.py:132
  42.7 11.4 %all_to_all.11.parts_ref = f32[32,4,128]{2,1,0:T(4,128)} all-to-all(f32[32,4,128]{2,1,0:T(4,128)S(1)} %image.1), channel_id=1, replica_groups=mesh['band'=8,'gblk'=4] {'band','gblk'}, dimensions={0} | all-to-all | bytes 131072 | tf_op jit(solution)/shard_map/all_to_all | solution.py:148
  54.1 1.6 %final.1 = f32[2,2,1,2]{3,2,1,0:T(1,128)} custom-call(f32[32,4,128]{2,1,0:T(4,128)} %all_to_all.11.parts_ref), custom_call_target="tpu_custom_call" | custom-call | tf_op jit(solution)/shard_map/final/pallas_call | solution.py:149
